TPU v7x, 32 devices: a whole 2x2x4 slice. The times are simulated.
32 devices in a mesh: rep: 1, fsdp: 32 (over z, y, x, core).
Axes of the slice: x: 2, y: 2, z: 4, core: 2. Of those that a mesh axis runs over, the one named last changes fastest.
Arguments:
- grads: bfloat16 [1, 24, 1280, 1280], P('rep', None, 'fsdp'), as said below
- group_counts: int32 [2], replicated, may hold values from 1 to 18, 24 in all
- owners: int32 [24], replicated, may hold values from 0 to 31, as said below
- left_stat: float32 [32, 1280, 1280], P('fsdp', 'rep'), may hold values from -4 to 4
- right_stat: float32 [32, 1280, 1280], P('fsdp', 'rep'), may hold values from -4 to 4
- left_root: bfloat16 [32, 1280, 1280], P('fsdp', 'rep'), as said below
- right_root: bfloat16 [32, 1280, 1280], P('fsdp', 'rep'), as said below
Outputs:
- left_new: float32 [32, 1280, 1280], P('fsdp', 'rep')
- right_new: float32 [32, 1280, 1280], P('fsdp', 'rep')
- update: bfloat16 [24, 1280, 1280], P(None, ('rep', 'fsdp'))
Inputs may be any that keep to these rules, and one draw needn't show every extreme that they name: `grads`: block gradients of every replica group, real-valued. `owners`: no slot is named by two blocks. `group_counts`: the counts add up to 24. `left_root`: Symmetric, with a positive diagonal of about 0.5 to 2, each entry within a small symmetric perturbation of that range, and off-diagonal entries much smaller than the diagonal. `right_root`: Symmetric, with a positive diagonal of about 0.5 to 2, each entry within a small symmetric perturbation of that range, and off-diagonal entries much smaller than the diagonal.
All inputs are finite; a program needn't handle non-finite values.
Results may differ from a plain program's by a relative error of at most 0.00065.
The roundings to bfloat16 on the way count: a program that leaves them out, or rounds other values in their place, can miss the bound.
Values may be sent and summed in bfloat16 or wider, within the bound.
A program may use at most 128 MiB of HBM per device.

v0:
```python
import jax
import jax.numpy as jnp
from jax import lax
from jax.sharding import PartitionSpec as P

BETA = 0.95
EPSILON = 1e-06


def on_device(grads, group_counts, owners, left_stat, right_stat, left_root, right_root):
    slots = lax.axis_size("fsdp")
    width = left_stat.shape[2]
    half_rows = left_stat.shape[1]
    slot_ids = jnp.arange(slots, dtype=jnp.int32)
    placing = (owners[:, None] == slot_ids[None, :]).astype(jnp.bfloat16)
    local = grads[0]
    summed = lax.psum(local, "rep").astype(jnp.float32).astype(jnp.bfloat16)
    slotted = jnp.einsum("bs,brc->src", placing, summed, preferred_element_type=jnp.float32).astype(
        jnp.bfloat16
    )
    block = lax.all_to_all(slotted, "fsdp", split_axis=0, concat_axis=1, tiled=True)[0]
    first = lax.axis_index("rep") * half_rows
    mine = lax.dynamic_slice_in_dim(block, first, half_rows, 0)
    columns = lax.dynamic_slice_in_dim(block, first, half_rows, 1)
    coef = (1.0 - BETA) / width
    left_gram = jnp.dot(mine, block.T, preferred_element_type=jnp.float32)
    right_gram = lax.dot_general(
        columns, block, (((0,), (0,)), ((), ())), preferred_element_type=jnp.float32
    )
    left_new = BETA * left_stat[0] + coef * left_gram
    right_new = BETA * right_stat[0] + coef * right_gram
    whole_root = lax.all_gather(right_root, "rep", axis=1, tiled=True)[0]
    halfway = jnp.dot(left_root[0], block, preferred_element_type=jnp.float32).astype(jnp.bfloat16)
    precond = jnp.dot(halfway, whole_root, preferred_element_type=jnp.float32)
    ends = jnp.cumsum(group_counts)
    starts = ends - group_counts
    block_ids = jnp.arange(owners.shape[0], dtype=jnp.int32)
    member = (
        (block_ids[:, None] >= starts[None, :]) & (block_ids[:, None] < ends[None, :])
    ).astype(jnp.float32)
    owned_here = (owners == lax.axis_index("fsdp")).astype(jnp.float32)
    my_groups = jnp.sum(owned_here[:, None] * member, axis=0)
    mine_float = mine.astype(jnp.float32)
    grad_part = my_groups * jnp.sum(mine_float * mine_float)
    prec_part = my_groups * jnp.sum(precond * precond)
    grad_sq, prec_sq = lax.psum((grad_part, prec_part), ("rep", "fsdp"))
    ratio = jnp.sum(my_groups * jnp.sqrt((grad_sq + EPSILON) / (prec_sq + EPSILON)))
    scaled = (precond * ratio).astype(jnp.bfloat16)
    returned = lax.all_to_all(scaled[None], "fsdp", split_axis=1, concat_axis=0, tiled=True)
    update = jnp.einsum(
        "bs,srw->brw", placing, returned, preferred_element_type=jnp.float32
    ).astype(jnp.bfloat16)
    return (left_new[None], right_new[None], update)


def solution(mesh):
    in_specs = (
        P("rep", None, "fsdp", None),
        P(),
        P(),
        P("fsdp", "rep", None),
        P("fsdp", "rep", None),
        P("fsdp", "rep", None),
        P("fsdp", "rep", None),
    )
    out_specs = (P("fsdp", "rep", None), P("fsdp", "rep", None), P(None, ("rep", "fsdp"), None))
    return jax.shard_map(
        on_device, mesh=mesh, in_specs=in_specs, out_specs=out_specs, check_vma=False
    )
```

profile of v0, /device:TPU:0, one launch (start us, length us, event | category | flops | bytes accessed | tf_op | source)
XLA Modules:
  0.0 352.4 jit_solution(14322082575381790667)
XLA Ops:
  0.6 0.0 copy-start
  0.6 3.0 convolution_convert_fusion.1
  3.6 3.5 copy.33
  7.1 0.0 copy-start.3
  7.1 0.0 copy-start.2
  7.1 7.9 %all-to-all-start = ((bf16[32,40,1280]{2,1,0:T(8,128)(2,1)}), bf16[32,40,1280]{2,1,0:T(8,128)(2,1)}, u32[]{:S(2)}, u32[]{:S(2)}) async-start(bf16[32,40,1280]{2,1,0:T(8,128)(2,1)} %copy.33), calls=%async_computation | async-start | bytes 6553600 | tf_op jit(solution)/shard_map/all_to_all | solution.py:21
  15.1 0.0 copy-done.3
  15.1 0.2 reduce-window.8
  15.2 0.0 copy-done.2
  15.3 0.2 fusion.18
  15.4 73.3 %all-to-all-done = bf16[32,40,1280]{2,1,0:T(8,128)(2,1)} async-done(((bf16[32,40,1280]{2,1,0:T(8,128)(2,1)}), bf16[32,40,1280]{2,1,0:T(8,128)(2,1)}, u32[]{:S(2)}, u32[]{:S(2)}) %all-to-all-start) | async-done | bytes 3276832 | tf_op jit(solution)/shard_map/all_to_all | solution.py:21
  88.7 0.0 copy-done
  88.7 23.3 %multiply_reduce_fusion = (f32[]{:T(128)}, f32[1280,1280]{1,0:T(8,128)}) fusion(bf16[1,1280,1280]{2,1,0:T(8,128)(2,1)S(1)} %copy-done, bf16[1280,1280]{1,0:T(8,128)(2,1)} %bitcast.3, bf16[1,1280,1280]{2,1,0:T(8,128)(2,1)} %param.12), kind=kOutput, calls=%fused_computation.9 | convolution fusion | flops 8393523200 | bytes 16384004 | tf_op jit(solution)/shard_map/dot_general | solution.py:34
  112.0 4.2 %multiply_reduce_fusion.1 = f32[]{:T(128)} fusion(bf16[32,40,1280]{2,1,0:T(8,128)(2,1)} %all-to-all-done), kind=kLoop, calls=%fused_computation.10 | loop fusion | flops 4915199 | bytes 3276804 | tf_op jit(solution)/shard_map/reduce_sum | solution.py:44
  116.2 1.3 broadcast_multiply_fusion.1
  117.5 38.1 %all-reduce = (f32[2]{0:T(128)S(1)}, f32[2]{0:T(128)S(1)}) all-reduce(f32[2]{0:T(128)S(1)} %get-tuple-element.21, f32[2]{0:T(128)S(1)} %get-tuple-element.20), channel_id=1, replica_groups=mesh['rep'=1,'fsdp'=32] {'rep','fsdp'}, use_global_device_ids=true, to_apply=%region_5.6 | all-reduce | flops 4 | bytes 32 | tf_op jit(solution)/shard_map/psum | solution.py:46
  155.6 0.6 multiply_reduce_fusion.2
  156.3 4.0 %fusion.5 = bf16[1,1280,1280]{2,1,0:T(8,128)(2,1)S(1)} fusion(f32[1280,1280]{1,0:T(8,128)} %get-tuple-element.23, f32[]{:T(128)} %multiply_reduce_fusion.2), kind=kLoop, calls=%fused_computation.13 | loop fusion | flops 3276800 | bytes 9830404 | tf_op jit(solution)/shard_map/broadcast_in_dim | solution.py:49
  160.3 21.5 %copy.43 = bf16[1,1280,1280]{2,0,1:T(2,128)(2,1)} copy(bf16[1,1280,1280]{2,1,0:T(8,128)(2,1)S(1)} %fusion.5) | data formatting | bytes 6553600 | tf_op jit(solution)/shard_map/broadcast_in_dim | solution.py:49
  181.7 0.5 broadcast.28
  182.2 69.6 %reduce.1 = bf16[1280,1280]{1,0:T(8,128)(2,1)S(1)} reduce(bf16[1280,1,1280]{2,1,0:T(2,128)(2,1)} %bitcast.49, bf16[]{:T(256)} %broadcast.28), dimensions={1}, to_apply=%bitcast.48.reduce_sub_computation | reduce | bytes 6553602
  251.8 2.5 reshape.47
  254.3 5.2 %all-to-all-start.1 = ((bf16[32,2,25600]{2,1,0:T(2,128)(2,1)}), bf16[32,2,25600]{2,1,0:T(2,128)(2,1)S(1)}, u32[]{:S(2)}, u32[]{:S(2)}) async-start(bf16[32,2,25600]{2,1,0:T(2,128)(2,1)} %reshape.47), calls=%async_computation.1 | async-start | bytes 6553600 | tf_op jit(solution)/shard_map/all_to_all | solution.py:49
  259.6 12.2 %fusion.1 = f32[1,1280,1280]{2,1,0:T(8,128)} fusion(bf16[1280,1280]{1,0:T(8,128)(2,1)} %bitcast.3, f32[1,1280,1280]{2,1,0:T(8,128)} %param.10), kind=kOutput, calls=%fused_computation.2 | convolution fusion | flops 4199219200 | bytes 16384000 | tf_op jit(solution)/shard_map/dot_general | solution.py:26
  271.8 12.3 %fusion.4 = f32[1,1280,1280]{2,1,0:T(8,128)} fusion(bf16[32,40,1280]{2,1,0:T(8,128)(2,1)} %all-to-all-done, f32[1,1280,1280]{2,1,0:T(8,128)} %param.11), kind=kOutput, calls=%fused_computation.6 | convolution fusion | flops 4199219200 | bytes 16384000 | tf_op jit(solution)/shard_map/dot_general | solution.py:27
  284.1 49.6 %all-to-all-done.1 = bf16[32,2,25600]{2,1,0:T(2,128)(2,1)S(1)} async-done(((bf16[32,2,25600]{2,1,0:T(2,128)(2,1)}), bf16[32,2,25600]{2,1,0:T(2,128)(2,1)S(1)}, u32[]{:S(2)}, u32[]{:S(2)}) %all-to-all-start.1) | async-done | bytes 3276832 | tf_op jit(solution)/shard_map/all_to_all | solution.py:49
  333.7 12.3 %reshape.48 = bf16[1280,1,1280]{2,1,0:T(2,128)(2,1)} reshape(bf16[32,2,25600]{2,1,0:T(2,128)(2,1)S(1)} %all-to-all-done.1) | data formatting | bytes 6553600
  346.0 3.4 copy.37
  349.4 0.0 copy-start.1
  349.4 0.9 convolution_convert_fusion.2
  350.2 1.9 copy.36
  352.1 0.0 copy-done.1
  (2 shorter events, 0.0 us)
Async XLA Ops:
  0.6 88.1 %copy-start = (bf16[1,1280,1280]{2,1,0:T(8,128)(2,1)S(1)}, bf16[1,1280,1280]{2,1,0:T(8,128)(2,1)}, u32[]{:S(2)}) copy-start(bf16[1,1280,1280]{2,1,0:T(8,128)(2,1)} %param.13) | copy-start | bytes 9830404
  7.1 7.9 %copy-start.3 = (s32[2]{0:T(128)S(1)}, s32[2]{0:T(128)}, u32[]{:S(2)}) copy-start(s32[2]{0:T(128)} %param.8) | copy-start | bytes 28
  7.1 8.1 %copy-start.2 = (s32[24]{0:T(128)S(1)}, s32[24]{0:T(128)}, u32[]{:S(2)}) copy-start(s32[24]{0:T(128)} %param.9) | copy-start | bytes 292
  7.1 81.6 %all-to-all-start = ((bf16[32,40,1280]{2,1,0:T(8,128)(2,1)}), bf16[32,40,1280]{2,1,0:T(8,128)(2,1)}, u32[]{:S(2)}, u32[]{:S(2)}) async-start(bf16[32,40,1280]{2,1,0:T(8,128)(2,1)} %copy.33), calls=%async_computation | async-start | bytes 6553600 | tf_op jit(solution)/shard_map/all_to_all | solution.py:21
  254.3 79.4 %all-to-all-start.1 = ((bf16[32,2,25600]{2,1,0:T(2,128)(2,1)}), bf16[32,2,25600]{2,1,0:T(2,128)(2,1)S(1)}, u32[]{:S(2)}, u32[]{:S(2)}) async-start(bf16[32,2,25600]{2,1,0:T(2,128)(2,1)} %reshape.47), calls=%async_computation.1 | async-start | bytes 6553600 | tf_op jit(solution)/shard_map/all_to_all | solution.py:49
  349.4 2.8 copy-start.1
where the time goes:
time: 356 us; the launch traced here: 352 us
  waiting for transfers between devices  123 us (35%)
  other arithmetic  80 us (22%)
  matrix products  51.7 us (15%)
  local copies, waits for them, and re-layouts  45.6 us (13%)
  blocking collectives  38.1 us (11%)
  starting transfers between devices  13.1 us (4%)
    all_to_all x1, waiting for transfers between devices, on_device(): lax.all_to_all(slotted, 'fsdp', split_axis=0, concat_axis=1, tiled=True)[0]  73.3 us
    unnamed x1, other arithmetic  69.6 us
    all_to_all x1, waiting for transfers between devices, on_device(): lax.all_to_all(scaled[None], 'fsdp', split_axis=1, concat_axis=0, tiled=T...  49.6 us
    psum x1, blocking collectives, on_device(): grad_sq, prec_sq = lax.psum((grad_part, prec_part), ('rep', 'fsdp'))  38.1 us
    dot_general x1, matrix products, on_device(): precond = jnp.dot(halfway, whole_root, preferred_element_type=jnp.float32)  23.3 us
    broadcast_in_dim x1, local copies, waits for them, and re-layouts, on_device(): scaled[None]  21.5 us
    unnamed x13, local copies, waits for them, and re-layouts  20.6 us
    dot_general x1, matrix products, on_device(): lax.dot_general(columns, block, (((0,), (0,)), ((), ())), preferred_eleme...  12.3 us
  transfers between devices with their start and end apart: 2, of which 2 were waited for; matrix products, arithmetic and copies ran while one was open for 7% of the time, Pallas kernels for 0%

commit v1 on v0

--- a/solution.py
+++ b/solution.py
@@ -46,7 +46,12 @@
     grad_sq, prec_sq = lax.psum((grad_part, prec_part), ("rep", "fsdp"))
     ratio = jnp.sum(my_groups * jnp.sqrt((grad_sq + EPSILON) / (prec_sq + EPSILON)))
     scaled = (precond * ratio).astype(jnp.bfloat16)
-    returned = lax.all_to_all(scaled[None], "fsdp", split_axis=1, concat_axis=0, tiled=True)
+    returned = jnp.concatenate(
+        lax.all_to_all(
+            jnp.stack(jnp.split(scaled[None], lax.axis_size("fsdp"), axis=1)), "fsdp", 0, 0
+        ),
+        axis=0,
+    )
     update = jnp.einsum(
         "bs,srw->brw", placing, returned, preferred_element_type=jnp.float32
     ).astype(jnp.bfloat16)

time: 356 us -> 265 us (0.74); the launches traced: 352 us -> 265 us
  other arithmetic: 80 us -> 10.5 us
  local copies, waits for them, and re-layouts: 45.6 us -> 26.1 us
    unnamed x1 -> x0, other arithmetic: 69.6 us -> none
    broadcast_in_dim x1 -> x0, local copies, waits for them, and re-layouts: 21.5 us -> none  [on_device(): scaled[None]]
    unnamed x13 -> x38, local copies, waits for them, and re-layouts: 20.6 us -> 21.9 us
  transfers between devices with their start and end apart: 2 -> 2, of which waited for: 2 -> 2; matrix products, arithmetic and copies ran while one was open for 7% -> 9% of each run, Pallas kernels for 0% -> 0%
where the time goes in v1:
time: 265 us
  waiting for transfers between devices  123 us (46%)
  matrix products  53.6 us (20%)
  blocking collectives  38.1 us (14%)
  local copies, waits for them, and re-layouts  26.1 us (10%)
  starting transfers between devices  12.7 us (5%)
  other arithmetic  10.5 us (4%)
    all_to_all x1, waiting for transfers between devices, on_device(): lax.all_to_all(slotted, 'fsdp', split_axis=0, concat_axis=1, tiled=True)[0]  73.6 us
    all_to_all x1, waiting for transfers between devices, on_device(): lax.all_to_all(jnp.stack(jnp.split(scaled[None], lax.axis_size('fsdp'), a...  49.6 us
    psum x1, blocking collectives, on_device(): grad_sq, prec_sq = lax.psum((grad_part, prec_part), ('rep', 'fsdp'))  38.1 us
    dot_general x1, matrix products, on_device(): precond = jnp.dot(halfway, whole_root, preferred_element_type=jnp.float32)  23.4 us
    unnamed x38, local copies, waits for them, and re-layouts  21.9 us
    dot_general x1, matrix products, on_device(): lax.dot_general(columns, block, (((0,), (0,)), ((), ())), preferred_eleme...  12.3 us
    dot_general x1, matrix products, on_device(): left_gram = jnp.dot(mine, block.T, preferred_element_type=jnp.float32)  12.2 us
    all_to_all x1, starting transfers between devices, on_device(): lax.all_to_all(slotted, 'fsdp', split_axis=0, concat_axis=1, tiled=True)[0]  7.62 us
  transfers between devices with their start and end apart: 2, of which 2 were waited for; matrix products, arithmetic and copies ran while one was open for 9% of the time, Pallas kernels for 0%

profile of v1, /device:TPU:0, one launch (start us, length us, event | category | flops | bytes accessed | tf_op | source)
XLA Modules:
  0.0 264.9 jit_solution(521083990299174122)
XLA Ops:
  0.6 3.0 %convolution_convert_fusion.1 = bf16[32,40,1280]{2,0,1:T(8,128)(2,1)S(1)} fusion(bf16[24,40,1280]{2,1,0:T(8,128)(2,1)} %bitcast.173, s32[24]{0:T(128)} %param.9), kind=kOutput, calls=%fused_computation.11 | convolution fusion | flops 80282368 | bytes 5734496 | tf_op jit(solution)/shard_map/bs,brc->src/dot_general | solution.py:18
  3.6 3.5 %copy.28 = bf16[32,40,1280]{2,1,0:T(8,128)(2,1)} copy(bf16[32,40,1280]{2,0,1:T(8,128)(2,1)S(1)} %convolution_convert_fusion.1) | data formatting | bytes 6553600 | tf_op jit(solution)/shard_map/convert_element_type | solution.py:18
  7.1 7.6 %all-to-all-start = ((bf16[32,40,1280]{2,1,0:T(8,128)(2,1)}), bf16[32,40,1280]{2,1,0:T(8,128)(2,1)}, u32[]{:S(2)}, u32[]{:S(2)}) async-start(bf16[32,40,1280]{2,1,0:T(8,128)(2,1)} %copy.28), calls=%async_computation | async-start | bytes 6553600 | tf_op jit(solution)/shard_map/all_to_all | solution.py:21
  15.2 73.6 %all-to-all-done = bf16[32,40,1280]{2,1,0:T(8,128)(2,1)} async-done(((bf16[32,40,1280]{2,1,0:T(8,128)(2,1)}), bf16[32,40,1280]{2,1,0:T(8,128)(2,1)}, u32[]{:S(2)}, u32[]{:S(2)}) %all-to-all-start) | async-done | bytes 3276832 | tf_op jit(solution)/shard_map/all_to_all | solution.py:21
  88.7 23.4 %multiply_reduce_fusion = (f32[]{:T(128)}, f32[1280,1280]{1,0:T(8,128)}) fusion(bf16[1,1280,1280]{2,1,0:T(8,128)(2,1)S(1)} %copy-done, bf16[1280,1280]{1,0:T(8,128)(2,1)} %bitcast.3, bf16[1,1280,1280]{2,1,0:T(8,128)(2,1)} %param.12), kind=kOutput, calls=%fused_computation.9 | convolution fusion | flops 8393523200 | bytes 16384004 | tf_op jit(solution)/shard_map/dot_general | solution.py:34
  112.1 4.2 %multiply_reduce_fusion.1 = f32[]{:T(128)} fusion(bf16[32,40,1280]{2,1,0:T(8,128)(2,1)} %all-to-all-done), kind=kLoop, calls=%fused_computation.10 | loop fusion | flops 4915199 | bytes 3276804 | tf_op jit(solution)/shard_map/reduce_sum | solution.py:44
  116.3 1.3 broadcast_multiply_fusion.1
  117.6 38.1 %all-reduce = (f32[2]{0:T(128)S(1)}, f32[2]{0:T(128)S(1)}) all-reduce(f32[2]{0:T(128)S(1)} %get-tuple-element.18, f32[2]{0:T(128)S(1)} %get-tuple-element.17), channel_id=1, replica_groups=mesh['rep'=1,'fsdp'=32] {'rep','fsdp'}, use_global_device_ids=true, to_apply=%region_5.6 | all-reduce | flops 4 | bytes 32 | tf_op jit(solution)/shard_map/psum | solution.py:46
  156.3 4.0 %fusion.5 = bf16[1,1280,1280]{2,1,0:T(8,128)(2,1)S(1)} fusion(f32[1280,1280]{1,0:T(8,128)} %get-tuple-element.20, f32[]{:T(128)} %multiply_reduce_fusion.2), kind=kLoop, calls=%fused_computation.13 | loop fusion | flops 3276800 | bytes 9830404 | tf_op jit(solution)/shard_map/broadcast_in_dim | solution.py:51
  160.9 0.7 fusion.43
  162.2 0.7 fusion.41
  162.9 0.6 fusion.40
  164.8 0.6 fusion.37
  165.5 0.6 fusion.36
  166.8 0.7 fusion.34
  169.3 0.7 fusion.30
  170.0 0.6 fusion.29
  171.3 0.7 fusion.27
  171.9 0.7 fusion.26
  175.1 0.6 fusion.21
  176.4 0.7 fusion.19
  177.1 0.7 fusion.18
  177.7 0.7 fusion.17
  178.4 0.6 fusion.16
  179.0 0.6 fusion.15
  179.7 0.7 fusion.14
  181.0 5.1 %all-to-all-start.1 = ((bf16[32,1,40,1280]{3,2,1,0:T(8,128)(2,1)}), bf16[32,1,40,1280]{3,2,1,0:T(8,128)(2,1)}, u32[]{:S(2)}, u32[]{:S(2)}) async-start(bf16[32,1,40,1280]{3,2,1,0:T(8,128)(2,1)} %fusion.13), calls=%async_computation.1 | async-start | bytes 6553600 | tf_op jit(solution)/shard_map/all_to_all | solution.py:50
  186.1 12.2 %fusion.1 = f32[1,1280,1280]{2,1,0:T(8,128)} fusion(bf16[1280,1280]{1,0:T(8,128)(2,1)} %bitcast.3, f32[1,1280,1280]{2,1,0:T(8,128)} %param.10), kind=kOutput, calls=%fused_computation.2 | convolution fusion | flops 4199219200 | bytes 16384000 | tf_op jit(solution)/shard_map/dot_general | solution.py:26
  198.3 12.3 %fusion.4 = f32[1,1280,1280]{2,1,0:T(8,128)} fusion(bf16[32,40,1280]{2,1,0:T(8,128)(2,1)} %all-to-all-done, f32[1,1280,1280]{2,1,0:T(8,128)} %param.11), kind=kOutput, calls=%fused_computation.6 | convolution fusion | flops 4199219200 | bytes 16384000 | tf_op jit(solution)/shard_map/dot_general | solution.py:27
  210.6 49.6 %all-to-all-done.1 = bf16[32,1,40,1280]{3,2,1,0:T(8,128)(2,1)} async-done(((bf16[32,1,40,1280]{3,2,1,0:T(8,128)(2,1)}), bf16[32,1,40,1280]{3,2,1,0:T(8,128)(2,1)}, u32[]{:S(2)}, u32[]{:S(2)}) %all-to-all-start.1) | async-done | bytes 3276832 | tf_op jit(solution)/shard_map/all_to_all | solution.py:50
  260.2 2.8 %convolution_convert_fusion.2 = bf16[24,40,1280]{2,0,1:T(8,128)(2,1)S(1)} fusion(bf16[32,40,1280]{2,1,0:T(8,128)(2,1)} %bitcast.45, s32[24]{0:T(128)S(1)} %copy-done.1), kind=kOutput, calls=%fused_computation.12 | convolution fusion | flops 79872768 | bytes 5734496 | tf_op jit(solution)/shard_map/bs,srw->brw/dot_general | solution.py:55
  263.0 1.9 copy.30
  (26 shorter events, 10.6 us)
Async XLA Ops:
  0.6 88.1 %copy-start = (bf16[1,1280,1280]{2,1,0:T(8,128)(2,1)S(1)}, bf16[1,1280,1280]{2,1,0:T(8,128)(2,1)}, u32[]{:S(2)}) copy-start(bf16[1,1280,1280]{2,1,0:T(8,128)(2,1)} %param.13) | copy-start | bytes 9830404
  7.1 7.6 %copy-start.2 = (s32[2]{0:T(128)S(1)}, s32[2]{0:T(128)}, u32[]{:S(2)}) copy-start(s32[2]{0:T(128)} %param.8) | copy-start | bytes 28
  7.1 7.8 %copy-start.1 = (s32[24]{0:T(128)S(1)}, s32[24]{0:T(128)}, u32[]{:S(2)}) copy-start(s32[24]{0:T(128)} %param.9) | copy-start | bytes 292
  7.1 81.6 %all-to-all-start = ((bf16[32,40,1280]{2,1,0:T(8,128)(2,1)}), bf16[32,40,1280]{2,1,0:T(8,128)(2,1)}, u32[]{:S(2)}, u32[]{:S(2)}) async-start(bf16[32,40,1280]{2,1,0:T(8,128)(2,1)} %copy.28), calls=%async_computation | async-start | bytes 6553600 | tf_op jit(solution)/shard_map/all_to_all | solution.py:21
  181.0 79.3 %all-to-all-start.1 = ((bf16[32,1,40,1280]{3,2,1,0:T(8,128)(2,1)}), bf16[32,1,40,1280]{3,2,1,0:T(8,128)(2,1)}, u32[]{:S(2)}, u32[]{:S(2)}) async-start(bf16[32,1,40,1280]{3,2,1,0:T(8,128)(2,1)} %fusion.13), calls=%async_computation.1 | async-start | bytes 6553600 | tf_op jit(solution)/shard_map/all_to_all | solution.py:50
